TPU v7x, 32 devices: a whole 2x2x4 slice. The times are simulated.
32 devices in a mesh: sib: 4 (over y, x), wide: 8 (over z, core).
Axes of the slice: x: 2, y: 2, z: 4, core: 2. Of those that a mesh axis runs over, the one named last changes fastest.
Arguments:
- right_side: float32 [128, 8, 2048], P(None, 'wide', 'sib'), may hold values from -6 to 6
- tree_order: int32 [8, 2048], P('wide', 'sib'), may hold values from 0 to 2047, each once within a row
- x_start: float32 [128, 8, 2048], P(None, 'wide', 'sib'), may hold values from -6 to 6
- tangent_start: float32 [128, 8, 2048], P(None, 'wide', 'sib'), may hold values from -3 to 3
- dense_kernel: float32 [8, 4, 512, 512], P('wide', 'sib'), may hold values from -0.25 to 0.25
- dense_deriv: float32 [8, 4, 512, 512], P('wide', 'sib'), may hold values from -0.25 to 0.25
- leaf_basis: float32 [8, 4, 512, 256], P('wide', 'sib'), may hold values from -0.25 to 0.25
- transfer: float32 [8, 4, 256, 256], P('wide', 'sib'), may hold values from -0.375 to 0.375
- sibling_kernel: float32 [8, 4, 3, 256, 256], P('wide', 'sib'), may hold values from -0.21875 to 0.21875
- sibling_deriv: float32 [8, 4, 3, 256, 256], P('wide', 'sib'), may hold values from -0.21875 to 0.21875
- partner_list: int32 [8, 4], P('wide'), may hold values from 0 to 7, as said below
- parent_kernel: float32 [8, 4, 256, 256], P('wide'), may hold values from -0.1875 to 0.1875
- parent_deriv: float32 [8, 4, 256, 256], P('wide'), may hold values from -0.1875 to 0.1875
Outputs:
- solution: float32 [128, 8, 2048], P(None, 'wide', 'sib')
- tangent: float32 [128, 8, 2048], P(None, 'wide', 'sib')
Inputs may be any that keep to these rules, and one draw needn't show every extreme that they name: `partner_list`: row p names 4 different parent clusters, none of them p. `tree_order`: each row holds every position 0 .. 2047 once.
All inputs are finite; a program needn't handle non-finite values.
Results may differ from a plain program's by a relative error of at most 0.0001.
Values sent between devices are 32-bit elements; how exact they have to be, the bound alone decides.
No kernel may reach another device: no remote copies, remote signals or barrier semaphores. Data moves between devices by JAX's collectives and lax.ppermute only.
A program may use at most 64 MiB of HBM per device.

v0:
```python
import functools

import jax
import jax.numpy as jnp
from jax import lax
from jax.experimental import pallas as pl
from jax.experimental.pallas import tpu as pltpu
from jax.sharding import PartitionSpec as P


ITERS = 2
relax_step = 0.3
noise_level = 1.0
keep = 1.0 - relax_step * noise_level


GRANT = 24 * 1024 * 1024
LARGE = 61 * 1024 * 1024

f32 = jnp.float32
bf16 = jnp.bfloat16


def halves(value):
    high = value.astype(bf16)
    return high, (value - high.astype(f32)).astype(bf16)


def one_pass(left, right, contract):
    return lax.dot_general(left, right, (contract, ((), ())), preferred_element_type=f32)


def mm(left, right, contract=((1,), (0,))):
    return (
        one_pass(left[0], right[0], contract)
        + one_pass(left[0], right[1], contract)
        + one_pass(left[1], right[0], contract)
    )


def mm_t(left, right):
    return mm(left, right, ((1,), (1,)))


def rows_of(pair, start, size):
    return tuple(part[start : start + size] for part in pair)


VMEM = pl.BlockSpec(memory_space=pltpu.VMEM)
SMEM = pl.BlockSpec(memory_space=pltpu.SMEM)
HBM = pl.BlockSpec(memory_space=pltpu.HBM)


def call(kernel, inputs, outputs, flops, scratch=(), scalars=0, specs=None, kind=f32, grant=GRANT):
    if specs is None:
        specs = [SMEM] * scalars + [VMEM] * (len(inputs) - scalars)
    moved = sum(4 * item.size for item in inputs)
    return pl.pallas_call(
        kernel,
        in_specs=specs,
        out_specs=tuple(VMEM for _ in outputs),
        out_shape=tuple(jax.ShapeDtypeStruct(shape, kind) for shape in outputs),
        scratch_shapes=list(scratch),
        compiler_params=pltpu.CompilerParams(vmem_limit_bytes=grant),
        cost_estimate=pl.CostEstimate(flops=3 * flops, bytes_accessed=moved, transcendentals=0),
    )(*inputs)


def peer(o):
    return lax.bitwise_xor(lax.axis_index("sib"), o)


def send_quarters(term, count, outs):
    rhs = term.shape[0] // 2
    part = rhs // count
    for o, out in enumerate(outs):
        row = pl.multiple_of(peer(o) * part, part)
        out[:part] = term[pl.ds(row, part)]
        out[part:] = term[pl.ds(pl.multiple_of(rhs + row, part), part)]


def start_kernel(count, *refs):
    loads, (xs_ref, ab_ref, *outs) = refs[:4], refs[4 : 6 + count]
    term, *held, done = refs[6 + count :]
    copies = [pltpu.make_async_copy(*ends, done.at[k]) for k, ends in enumerate(zip(loads, held))]
    for copy in copies:
        copy.start()
    for copy in copies:
        copy.wait()
    x_ref, dx_ref, basis_ref, trans_ref = held
    rhs = x_ref.shape[0]
    xs_ref[:rhs] = x_ref[:, 0, :]
    xs_ref[rhs:] = dx_ref[:, 0, :]
    ab = mm(halves(xs_ref[...]), halves(basis_ref[0, 0]))
    ab_ref[...] = ab
    term[...] = mm(halves(ab), halves(trans_ref[0, 0]))
    send_quarters(term, count, outs)


def local_kernel(xs_ref, dense_ref, deriv_ref, base_ref):
    rhs = xs_ref.shape[0] // 2
    xs = xs_ref[...]
    pair = halves(xs)
    image = mm(pair, halves(dense_ref[0, 0]))
    extra = mm(rows_of(pair, 0, rhs), halves(deriv_ref[0, 0]))
    base_ref[:rhs] = keep * xs[:rhs] - relax_step * image[:rhs]
    base_ref[rhs:] = keep * xs[rhs:] - relax_step * (image[rhs:] + extra)


def sum_kernel(*refs):
    total = refs[0][...]
    for ref in refs[1:-1]:
        total = total + ref[...]
    refs[-1][...] = total


def parent_kernel_body(wide, partners_ref, kern_ref, deriv_ref, *rest):
    *pieces, out, held = rest
    me = lax.axis_index("wide")
    at = 0
    for ref in pieces:
        for row in range(0, ref.shape[0], out.shape[0]):
            held[at] = ref[row : row + out.shape[0]]
            at += 1
    chosen = []
    for k in range(partners_ref.shape[1]):
        apart = lax.bitwise_xor(partners_ref[0, k], me)
        slot = lax.rem(apart, 2) * (wide // 2) + lax.div(apart, 2)
        chosen.append(held[slot])
    part = out.shape[0] // 2
    pair = halves(jnp.concatenate(chosen, axis=1))
    depth = pair[0].shape[1]
    kern = halves(kern_ref[0].reshape(depth, -1))
    deriv = halves(deriv_ref[0].reshape(depth, -1))
    field = mm(pair, kern)
    out[:part] = field[:part]
    out[part:] = field[part:] + mm(rows_of(pair, 0, part), deriv)


def grouped(sizes, refs):
    refs = iter(refs)
    return [[next(refs) for _ in range(size)] for size in sizes]


def sibling_body(sizes, kern_ref, deriv_ref, *rest):
    pieces, out = grouped(sizes, rest[:-1]), rest[-1]
    count = len(sizes) + 1
    me = lax.axis_index("sib")
    rhs = out.shape[0] // 2
    total = None
    extra = None
    for o in range(1, count):
        parts = [ref[...] for ref in pieces[o - 1]]
        value = parts[0] if len(parts) == 1 else jnp.concatenate(parts, axis=0)
        slot = lax.rem(peer(o) - me - 1 + count, count)
        pair = halves(value)
        term = mm(pair, halves(kern_ref[0, 0, slot]))
        more = mm(rows_of(pair, 0, rhs), halves(deriv_ref[0, 0, slot]))
        total = term if total is None else total + term
        extra = more if extra is None else extra + more
    out[:rhs] = total[:rhs]
    out[rhs:] = total[rhs:] + extra


def pick_body(count, order_ref, pick):
    columns = order_ref.shape[1]
    rows = pick.shape[0] // count
    chunk = 16
    place = lax.broadcasted_iota(jnp.int32, (chunk, columns), 0)
    for o in range(count):
        wanted = jnp.broadcast_to(order_ref[...] - peer(o) * rows, (chunk, columns)) - place
        for at in range(0, rows, chunk):
            pick[pl.ds(o * rows + at, chunk)] = jnp.where(wanted == at, 1.0, 0.0).astype(bf16)


def order_body(pick, *rest):
    pieces, (out, value) = rest[:-2], rest[-2:]
    rhs = out.shape[0]
    rows = pieces[0].shape[-1]
    for o, ref in enumerate(pieces):
        value[:, o * rows : (o + 1) * rows] = ref[:, 0, :]
    both = one_pass(jnp.concatenate(halves(value[...]), axis=0), pick[...], ((1,), (0,)))
    out[...] = both[:rhs] + both[rhs:]


def collect(count, pieces, whole):
    rhs = whole.shape[0] // 2
    part = rhs // count
    for o in range(count):
        row = pl.multiple_of(peer(o) * part, part)
        whole[pl.ds(row, part)] = pieces[o][:part]
        whole[pl.ds(pl.multiple_of(rhs + row, part), part)] = pieces[o][part:]


def weights_body(basis_ref, trans_ref, lift_ref, again_ref, term_ref):
    basis = halves(basis_ref[0, 0])
    trans = halves(trans_ref[0, 0])
    lift = mm(basis, trans)
    lift_ref[...] = lift
    again = mm(halves(lift), basis, ((0,), (0,)))
    again_ref[...] = again
    term_ref[...] = mm(halves(again), trans)


def before_body(last, basis_ref, trans_ref, near_ref, base_ref, right_ref, *outs):
    rhs = right_ref.shape[0]
    new_ref = outs[0]
    basis = halves(basis_ref[0, 0])
    new_ref[...] = base_ref[...] - relax_step * mm_t(halves(near_ref[...]), basis)
    new_ref[:rhs] = new_ref[:rhs] + relax_step * right_ref[...]
    if not last:
        ab = mm(halves(new_ref[...]), basis)
        outs[1][...] = ab
        outs[2][...] = mm(halves(ab), halves(trans_ref[0, 0]))


def terms_body(count, weight_ref, before_ref, *rest):
    pieces, rest = rest[:count], rest[count:]
    outs, (whole, term) = rest[:count], rest[count:]
    collect(count, pieces, whole)
    term[...] = before_ref[...] - relax_step * mm(halves(whole[...]), halves(weight_ref[...]))
    send_quarters(term, count, outs)


def coeffs_body(count, weight_ref, before_ref, *rest):
    pieces, (out, whole) = rest[:count], rest[count:]
    collect(count, pieces, whole)
    out[...] = before_ref[...] - relax_step * mm(halves(whole[...]), halves(weight_ref[...]))


def points_body(count, last, lift_ref, new_ref, *rest):
    pieces, (*outs, whole) = rest[:count], rest[count:]
    collect(count, pieces, whole)
    new = new_ref[...] - relax_step * mm_t(halves(whole[...]), halves(lift_ref[...]))
    if last:
        rhs = new.shape[0] // 2
        outs[0][:, 0, :] = new[:rhs]
        outs[1][:, 0, :] = new[rhs:]
    else:
        outs[0][...] = new


def join_body(*refs):
    for k, ref in enumerate(refs[:-1]):
        refs[-1][k * ref.shape[0] : (k + 1) * ref.shape[0]] = ref[...]


def body(
    right_side,
    tree_order,
    x_start,
    tangent_start,
    dense_kernel,
    dense_deriv,
    leaf_basis,
    transfer,
    sibling_kernel,
    sibling_deriv,
    partner_list,
    parent_kernel,
    parent_deriv,
):
    count = lax.axis_size("sib")
    wide = lax.axis_size("wide")
    rhs = x_start.shape[0]
    leaf = x_start.shape[2]
    rank = leaf_basis.shape[3]
    partners = partner_list.shape[1]
    part = rhs // count
    unit = 2 * rhs * rank * rank

    def sib_from(value, o):
        return lax.ppermute(value, "sib", [(i, i ^ o) for i in range(count)])

    def wide_from(value, k):
        return lax.ppermute(value, "wide", [(i, i ^ k) for i in range(wide)])

    quarter = (2 * part, rank)
    both = (2 * rhs, rank)
    points = (2 * rhs, leaf)
    depth = leaf // rank

    def siblings(values):
        got = {}
        for o in reversed(range(1, count)):
            got[o] = sib_from(values[o], o)
        return [got[o] for o in range(1, count)]

    loaded = (x_start, tangent_start, leaf_basis, transfer)
    xs, ab, *terms = call(
        functools.partial(start_kernel, count),
        loaded,
        (points, both) + (quarter,) * count,
        unit * (2 * depth + 2),
        scratch=[pltpu.VMEM(both, f32)]
        + [pltpu.VMEM(item.shape, f32) for item in loaded]
        + [pltpu.SemaphoreType.DMA((len(loaded),))],
        specs=[HBM] * len(loaded),
        grant=LARGE,
    )
    got_right = [right_side] + siblings([right_side] * count)
    lift, again_weight, term_weight = call(
        weights_body,
        (leaf_basis, transfer),
        ((leaf, rank), (rank, rank), (rank, rank)),
        unit * 4 * depth,
    )
    (pick,) = call(
        functools.partial(pick_body, count),
        (tree_order,),
        ((count * leaf, leaf),),
        unit * depth,
        kind=bf16,
    )
    right = None
    for step in range(ITERS):
        last = step == ITERS - 1
        got_terms = [terms[0]] + siblings(terms)
        (mine,) = call(sum_kernel, got_terms, (quarter,), unit // count)
        away = {}
        for k in reversed(range(1, wide // 2)):
            away[k] = wide_from(mine, 2 * k)
        away = [away[k] for k in range(1, wide // 2)]
        twin = wide_from(mine, 1)
        if not last:
            mine, ab = lax.optimization_barrier((mine, ab))
        got_ab = siblings([ab] * count)
        (joined,) = call(join_body, away, (((wide // 2 - 1) * 2 * part, rank),), unit // count)
        twins = wide_from(joined, 1)
        (base,) = call(
            local_kernel, (xs, dense_kernel, dense_deriv), (points,), unit * 3 * depth * depth
        )
        if right is None:
            (right,) = call(
                order_body,
                [pick] + got_right,
                ((rhs, leaf),),
                unit * depth * depth * count,
                scratch=(pltpu.VMEM((rhs, count * leaf), f32),),
            )
        (near,) = call(
            functools.partial(sibling_body, [1] * (count - 1)),
            [sibling_kernel, sibling_deriv] + got_ab,
            (both,),
            unit * 3 * (count - 1),
        )
        before = call(
            functools.partial(before_body, last),
            [leaf_basis, transfer, near, base, right],
            (points,) if last else (points, both, both),
            unit * 4 * depth,
        )
        (field,) = call(
            functools.partial(parent_kernel_body, wide),
            [partner_list, parent_kernel, parent_deriv, mine, joined, twin, twins],
            (quarter,),
            unit * 3 * partners // count,
            scratch=(pltpu.VMEM((wide,) + quarter, f32),),
            scalars=1,
        )
        got_field = [field] + siblings([field] * count)
        whole = pltpu.VMEM(both, f32)
        if not last:
            terms = call(
                functools.partial(terms_body, count),
                [term_weight, before[2]] + got_field,
                (quarter,) * count,
                unit * 2,
                scratch=(whole, whole),
            )
            (ab,) = call(
                functools.partial(coeffs_body, count),
                [again_weight, before[1]] + got_field,
                (both,),
                unit * 2,
                scratch=(whole,),
            )
        shape = ((rhs, 1, leaf),) * 2 if last else (points,)
        xs, *more = call(
            functools.partial(points_body, count, last),
            [lift, before[0]] + got_field,
            shape,
            unit * 2 * depth,
            scratch=(whole,),
        )
    return xs, more[0]


def solution(mesh):
    placed = (
        P(None, "wide", "sib"),
        P("wide", "sib"),
        P(None, "wide", "sib"),
        P(None, "wide", "sib"),
        P("wide", "sib", None, None),
        P("wide", "sib", None, None),
        P("wide", "sib", None, None),
        P("wide", "sib", None, None),
        P("wide", "sib", None, None, None),
        P("wide", "sib", None, None, None),
        P("wide", None),
        P("wide", None, None, None),
        P("wide", None, None, None),
    )
    return jax.shard_map(
        body,
        mesh=mesh,
        in_specs=placed,
        out_specs=(P(None, "wide", "sib"), P(None, "wide", "sib")),
        check_vma=False,
    )
```

profile of v0, /device:TPU:0, one launch (start us, length us, event | category | flops | bytes accessed | tf_op | source)
XLA Modules:
  0.0 71.6 jit_solution(8973389233765529009)
XLA Ops:
  0.7 3.0 %collective-permute-start.6 = (f32[128,1,512]{2,1,0:T(1,128)}, f32[128,1,512]{2,1,0:T(1,128)S(1)}, u32[]{:S(2)}, u32[]{:S(2)}) collective-permute-start(f32[128,1,512]{2,1,0:T(1,128)} %rest_0_.1), channel_id=1, source_target_pairs={{0,8},{8,0},{16,24},{24,16},{1,9},{9,1},{17,25},{25,17},{2,10},{10... | collective-permute-start | bytes 786440 | tf_op jit(solution)/shard_map/ppermute | solution.py:273
  3.7 1.5 %collective-permute-start.7 = (f32[128,1,512]{2,1,0:T(1,128)}, f32[128,1,512]{2,1,0:T(1,128)S(1)}, u32[]{:S(2)}, u32[]{:S(2)}) collective-permute-start(f32[128,1,512]{2,1,0:T(1,128)} %rest_0_.1), channel_id=1, source_target_pairs={{0,16},{8,24},{16,0},{24,8},{1,17},{9,25},{17,1},{25,9},{2,18},{10... | collective-permute-start | bytes 786440 | tf_op jit(solution)/shard_map/ppermute | solution.py:273
  5.2 2.7 %shard_map.141 = (f32[256,512]{1,0:T(8,128)}, f32[256,256]{1,0:T(8,128)}, f32[64,256]{1,0:T(8,128)}, f32[64,256]{1,0:T(8,128)}, f32[64,256]{1,0:T(8,128)}, /*index=5*/f32[64,256]{1,0:T(8,128)}) custom-call(f32[128,1,512]{2,1,0:T(1,128)} %refs_0_.1, f32[128,1,512]{2,1,0:T(1,128)} %refs_1_.1, f32[1,1,512,256]{3,2,1,0:T(8,128)} %basis_ref.5, ...), custom_call_target="tpu_custom_call" | custom-call | flops 301989888 | bytes 1310720 | tf_op jit(solution)/shard_map/pallas_call | solution.py:58
  8.6 2.9 %collective-permute-start.2 = (f32[64,256]{1,0:T(8,128)}, f32[64,256]{1,0:T(8,128)S(1)}, u32[]{:S(2)}, u32[]{:S(2)}) collective-permute-start(f32[64,256]{1,0:T(8,128)} %get-tuple-element.25), channel_id=1, source_target_pairs={{0,24},{8,16},{16,8},{24,0},{1,25},{9,17},{17,9},{25,1},{2,26},{10... | collective-permute-start | bytes 196616 | tf_op jit(solution)/shard_map/ppermute | solution.py:273
  11.5 1.4 %collective-permute-done.refs_1_ = f32[64,256]{1,0:T(8,128)S(1)} collective-permute-done((f32[64,256]{1,0:T(8,128)}, f32[64,256]{1,0:T(8,128)S(1)}, u32[]{:S(2)}, u32[]{:S(2)}) %collective-permute-start) | collective-permute-done | bytes 65568 | tf_op jit(solution)/shard_map/ppermute | solution.py:273
  12.9 1.6 %collective-permute-done.1.refs_2_ = f32[64,256]{1,0:T(8,128)S(1)} collective-permute-done((f32[64,256]{1,0:T(8,128)}, f32[64,256]{1,0:T(8,128)S(1)}, u32[]{:S(2)}, u32[]{:S(2)}) %collective-permute-start.1) | collective-permute-done | bytes 65568 | tf_op jit(solution)/shard_map/ppermute | solution.py:273
  15.3 2.6 %collective-permute-start.10 = (f32[64,256]{1,0:T(8,128)S(1)}, f32[64,256]{1,0:T(8,128)S(1)}, u32[]{:S(2)}, u32[]{:S(2)}) collective-permute-start(f32[64,256]{1,0:T(8,128)S(1)} %shard_map.142.rest_0_), channel_id=1, source_target_pairs={{0,4},{1,5},{2,6},{3,7},{4,0},{5,1},{6,2},{7,3},{8,12},{9,13},{10,... | collective-permute-start | bytes 196616 | tf_op jit(solution)/shard_map/ppermute | solution.py:276
  18.0 2.4 %collective-permute-start.8 = (f32[128,1,512]{2,1,0:T(1,128)}, f32[128,1,512]{2,1,0:T(1,128)S(1)}, u32[]{:S(2)}, u32[]{:S(2)}) collective-permute-start(f32[128,1,512]{2,1,0:T(1,128)} %rest_0_.1), channel_id=1, source_target_pairs={{0,24},{8,16},{16,8},{24,0},{1,25},{9,17},{17,9},{25,1},{2,26},{10... | collective-permute-start | bytes 786440 | tf_op jit(solution)/shard_map/ppermute | solution.py:273
  20.4 1.3 %collective-permute-start.11 = (f32[64,256]{1,0:T(8,128)S(1)}, f32[64,256]{1,0:T(8,128)S(1)}, u32[]{:S(2)}, u32[]{:S(2)}) collective-permute-start(f32[64,256]{1,0:T(8,128)S(1)} %shard_map.142.rest_0_), channel_id=1, source_target_pairs={{0,6},{1,7},{2,4},{3,5},{4,2},{5,3},{6,0},{7,1},{8,14},{9,15},{10,... | collective-permute-start | bytes 196616 | tf_op jit(solution)/shard_map/ppermute | solution.py:276
  22.7 3.9 %collective-permute-done.11.refs_2_ = f32[64,256]{1,0:T(8,128)S(1)} collective-permute-done((f32[64,256]{1,0:T(8,128)S(1)}, f32[64,256]{1,0:T(8,128)S(1)}, u32[]{:S(2)}, u32[]{:S(2)}) %collective-permute-start.11) | collective-permute-done | bytes 65568 | tf_op jit(solution)/shard_map/ppermute | solution.py:276
  27.6 2.5 %collective-permute-start.5 = (f32[256,256]{1,0:T(8,128)}, f32[256,256]{1,0:T(8,128)S(1)}, u32[]{:S(2)}, u32[]{:S(2)}) collective-permute-start(f32[256,256]{1,0:T(8,128)} %get-tuple-element.27), channel_id=1, source_target_pairs={{0,24},{8,16},{16,8},{24,0},{1,25},{9,17},{17,9},{25,1},{2,26},{10... | collective-permute-start | bytes 786440 | tf_op jit(solution)/shard_map/ppermute | solution.py:273
  31.2 1.2 %shard_map.140 = (f32[512,256]{1,0:T(8,128)S(1)}, f32[256,256]{1,0:T(8,128)S(1)}, f32[256,256]{1,0:T(8,128)S(1)}) custom-call(f32[1,1,512,256]{3,2,1,0:T(8,128)S(1)} %copy-done, f32[1,1,256,256]{3,2,1,0:T(8,128)S(1)} %copy-done.7), custom_call_target="tpu_custom_call" | custom-call | flops 402653184 | bytes 786432 | tf_op jit(solution)/shard_map/pallas_call | solution.py:58
  34.9 1.2 %shard_map.149.rest_0_ = f32[64,256]{1,0:T(8,128)S(1)} custom-call(s32[1,4]{1,0:T(1,128)S(1)} %copy-done.12, f32[1,4,256,256]{3,2,1,0:T(8,128)S(1)} %copy-done.3, f32[1,4,256,256]{3,2,1,0:T(8,128)S(1)} %copy-done.4, f32[64,256]{1,0:T(8,128)S(1)} %shard_map.142.rest_0_, f32[192,256]{1,0:T(8,128)S(1)} %shard_map.148.rest_1_, ...), custom_call_target="tpu_custom_call" | custom-call | flops 150994944 | bytes 2621456 | tf_op jit(solution)/shard_map/pallas_call | solution.py:58
  37.4 2.2 %collective-permute-start.16 = (f32[64,256]{1,0:T(8,128)S(1)}, f32[64,256]{1,0:T(8,128)S(1)}, u32[]{:S(2)}, u32[]{:S(2)}) collective-permute-start(f32[64,256]{1,0:T(8,128)S(1)} %shard_map.149.rest_0_), channel_id=1, source_target_pairs={{0,24},{8,16},{16,8},{24,0},{1,25},{9,17},{17,9},{25,1},{2,26},{10... | collective-permute-start | bytes 196616 | tf_op jit(solution)/shard_map/ppermute | solution.py:273
  43.0 1.9 %collective-permute-start.20 = (f32[64,256]{1,0:T(8,128)S(1)}, f32[64,256]{1,0:T(8,128)S(1)}, u32[]{:S(2)}, u32[]{:S(2)}) collective-permute-start(f32[64,256]{1,0:T(8,128)S(1)} %get-tuple-element.35), channel_id=1, source_target_pairs={{0,8},{8,0},{16,24},{24,16},{1,9},{9,1},{17,25},{25,17},{2,10},{10... | collective-permute-start | bytes 196616 | tf_op jit(solution)/shard_map/ppermute | solution.py:273
  47.4 2.0 %collective-permute-done.21.refs_2_ = f32[64,256]{1,0:T(8,128)S(1)} collective-permute-done((f32[64,256]{1,0:T(8,128)S(1)}, f32[64,256]{1,0:T(8,128)S(1)}, u32[]{:S(2)}, u32[]{:S(2)}) %collective-permute-start.21) | collective-permute-done | bytes 65568 | tf_op jit(solution)/shard_map/ppermute | solution.py:273
  49.4 1.5 %collective-permute-done.22.refs_3_ = f32[64,256]{1,0:T(8,128)S(1)} collective-permute-done((f32[64,256]{1,0:T(8,128)S(1)}, f32[64,256]{1,0:T(8,128)S(1)}, u32[]{:S(2)}, u32[]{:S(2)}) %collective-permute-start.22) | collective-permute-done | bytes 65568 | tf_op jit(solution)/shard_map/ppermute | solution.py:273
  51.0 2.8 %collective-permute-start.24 = (f32[64,256]{1,0:T(8,128)S(1)}, f32[64,256]{1,0:T(8,128)S(1)}, u32[]{:S(2)}, u32[]{:S(2)}) collective-permute-start(f32[64,256]{1,0:T(8,128)S(1)} %shard_map.156.rest_0_), channel_id=1, source_target_pairs={{0,4},{1,5},{2,6},{3,7},{4,0},{5,1},{6,2},{7,3},{8,12},{9,13},{10,... | collective-permute-start | bytes 196616 | tf_op jit(solution)/shard_map/ppermute | solution.py:276
  53.8 1.6 %collective-permute-start.25 = (f32[64,256]{1,0:T(8,128)S(1)}, f32[64,256]{1,0:T(8,128)S(1)}, u32[]{:S(2)}, u32[]{:S(2)}) collective-permute-start(f32[64,256]{1,0:T(8,128)S(1)} %shard_map.156.rest_0_), channel_id=1, source_target_pairs={{0,6},{1,7},{2,4},{3,5},{4,2},{5,3},{6,0},{7,1},{8,14},{9,15},{10,... | collective-permute-start | bytes 196616 | tf_op jit(solution)/shard_map/ppermute | solution.py:276
  57.1 2.2 %collective-permute-start.19 = (f32[256,256]{1,0:T(8,128)S(1)}, f32[256,256]{1,0:T(8,128)S(1)}, u32[]{:S(2)}, u32[]{:S(2)}) collective-permute-start(f32[256,256]{1,0:T(8,128)S(1)} %shard_map.150), channel_id=1, source_target_pairs={{0,24},{8,16},{16,8},{24,0},{1,25},{9,17},{17,9},{25,1},{2,26},{10... | collective-permute-start | bytes 786440 | tf_op jit(solution)/shard_map/ppermute | solution.py:273
  61.7 1.2 %shard_map.158.rest_0_ = f32[64,256]{1,0:T(8,128)S(1)} custom-call(s32[1,4]{1,0:T(1,128)S(1)} %copy-done.12, f32[1,4,256,256]{3,2,1,0:T(8,128)S(1)} %copy-done.3, f32[1,4,256,256]{3,2,1,0:T(8,128)S(1)} %copy-done.4, f32[64,256]{1,0:T(8,128)S(1)} %shard_map.156.rest_0_, f32[192,256]{1,0:T(8,128)S(1)} %shard_map.157.rest_1_, ...), custom_call_target="tpu_custom_call" | custom-call | flops 150994944 | bytes 2621456 | tf_op jit(solution)/shard_map/pallas_call | solution.py:58
  65.2 1.3 %collective-permute-start.30 = (f32[64,256]{1,0:T(8,128)S(1)}, f32[64,256]{1,0:T(8,128)S(1)}, u32[]{:S(2)}, u32[]{:S(2)}) collective-permute-start(f32[64,256]{1,0:T(8,128)S(1)} %shard_map.158.rest_0_), channel_id=1, source_target_pairs={{0,24},{8,16},{16,8},{24,0},{1,25},{9,17},{17,9},{25,1},{2,26},{10... | collective-permute-start | bytes 196616 | tf_op jit(solution)/shard_map/ppermute | solution.py:273
  69.0 1.3 %collective-permute-done.30.rest_3_ = f32[64,256]{1,0:T(8,128)S(1)} collective-permute-done((f32[64,256]{1,0:T(8,128)S(1)}, f32[64,256]{1,0:T(8,128)S(1)}, u32[]{:S(2)}, u32[]{:S(2)}) %collective-permute-start.30) | collective-permute-done | bytes 65568 | tf_op jit(solution)/shard_map/ppermute | solution.py:273
  70.4 1.2 %shard_map.159 = (f32[128,1,512]{2,1,0:T(1,128)}, f32[128,1,512]{2,1,0:T(1,128)}) custom-call(f32[512,256]{1,0:T(8,128)S(1)} %get-tuple-element.20.lift_ref, f32[256,512]{1,0:T(8,128)S(1)} %shard_map.154.new_ref, f32[64,256]{1,0:T(8,128)S(1)} %shard_map.158.rest_0_, f32[64,256]{1,0:T(8,128)S(1)} %collective-permute-done.28.rest_1_, ...), custom_call_target="tpu_custom_call" | custom-call | flops 201326592 | bytes 1310720 | tf_op jit(solution)/shard_map/pallas_call | solution.py:58
  (84 shorter events, 22.9 us)
Async XLA Ops:
  0.7 26.9 %collective-permute-start.6 = (f32[128,1,512]{2,1,0:T(1,128)}, f32[128,1,512]{2,1,0:T(1,128)S(1)}, u32[]{:S(2)}, u32[]{:S(2)}) collective-permute-start(f32[128,1,512]{2,1,0:T(1,128)} %rest_0_.1), channel_id=1, source_target_pairs={{0,8},{8,0},{16,24},{24,16},{1,9},{9,1},{17,25},{25,17},{2,10},{10... | collective-permute-start | bytes 786440 | tf_op jit(solution)/shard_map/ppermute | solution.py:273
  3.7 26.4 %collective-permute-start.7 = (f32[128,1,512]{2,1,0:T(1,128)}, f32[128,1,512]{2,1,0:T(1,128)S(1)}, u32[]{:S(2)}, u32[]{:S(2)}) collective-permute-start(f32[128,1,512]{2,1,0:T(1,128)} %rest_0_.1), channel_id=1, source_target_pairs={{0,16},{8,24},{16,0},{24,8},{1,17},{9,25},{17,1},{25,9},{2,18},{10... | collective-permute-start | bytes 786440 | tf_op jit(solution)/shard_map/ppermute | solution.py:273
  7.9 5.0 %collective-permute-start = (f32[64,256]{1,0:T(8,128)}, f32[64,256]{1,0:T(8,128)S(1)}, u32[]{:S(2)}, u32[]{:S(2)}) collective-permute-start(f32[64,256]{1,0:T(8,128)} %get-tuple-element.23), channel_id=1, source_target_pairs={{0,8},{8,0},{16,24},{24,16},{1,9},{9,1},{17,25},{25,17},{2,10},{10... | collective-permute-start | bytes 196616 | tf_op jit(solution)/shard_map/ppermute | solution.py:273
  8.5 5.9 %collective-permute-start.1 = (f32[64,256]{1,0:T(8,128)}, f32[64,256]{1,0:T(8,128)S(1)}, u32[]{:S(2)}, u32[]{:S(2)}) collective-permute-start(f32[64,256]{1,0:T(8,128)} %get-tuple-element.24), channel_id=1, source_target_pairs={{0,16},{8,24},{16,0},{24,8},{1,17},{9,25},{17,1},{25,9},{2,18},{10... | collective-permute-start | bytes 196616 | tf_op jit(solution)/shard_map/ppermute | solution.py:273
  8.6 5.9 %collective-permute-start.2 = (f32[64,256]{1,0:T(8,128)}, f32[64,256]{1,0:T(8,128)S(1)}, u32[]{:S(2)}, u32[]{:S(2)}) collective-permute-start(f32[64,256]{1,0:T(8,128)} %get-tuple-element.25), channel_id=1, source_target_pairs={{0,24},{8,16},{16,8},{24,0},{1,25},{9,17},{17,9},{25,1},{2,26},{10... | collective-permute-start | bytes 196616 | tf_op jit(solution)/shard_map/ppermute | solution.py:273
  15.3 6.4 %collective-permute-start.10 = (f32[64,256]{1,0:T(8,128)S(1)}, f32[64,256]{1,0:T(8,128)S(1)}, u32[]{:S(2)}, u32[]{:S(2)}) collective-permute-start(f32[64,256]{1,0:T(8,128)S(1)} %shard_map.142.rest_0_), channel_id=1, source_target_pairs={{0,4},{1,5},{2,6},{3,7},{4,0},{5,1},{6,2},{7,3},{8,12},{9,13},{10,... | collective-permute-start | bytes 196616 | tf_op jit(solution)/shard_map/ppermute | solution.py:276
  18.0 15.4 %collective-permute-start.8 = (f32[128,1,512]{2,1,0:T(1,128)}, f32[128,1,512]{2,1,0:T(1,128)S(1)}, u32[]{:S(2)}, u32[]{:S(2)}) collective-permute-start(f32[128,1,512]{2,1,0:T(1,128)} %rest_0_.1), channel_id=1, source_target_pairs={{0,24},{8,16},{16,8},{24,0},{1,25},{9,17},{17,9},{25,1},{2,26},{10... | collective-permute-start | bytes 786440 | tf_op jit(solution)/shard_map/ppermute | solution.py:273
  20.4 6.2 %collective-permute-start.11 = (f32[64,256]{1,0:T(8,128)S(1)}, f32[64,256]{1,0:T(8,128)S(1)}, u32[]{:S(2)}, u32[]{:S(2)}) collective-permute-start(f32[64,256]{1,0:T(8,128)S(1)} %shard_map.142.rest_0_), channel_id=1, source_target_pairs={{0,6},{1,7},{2,4},{3,5},{4,2},{5,3},{6,0},{7,1},{8,14},{9,15},{10,... | collective-permute-start | bytes 196616 | tf_op jit(solution)/shard_map/ppermute | solution.py:276
  21.7 5.4 %collective-permute-start.9 = (f32[64,256]{1,0:T(8,128)S(1)}, f32[64,256]{1,0:T(8,128)S(1)}, u32[]{:S(2)}, u32[]{:S(2)}) collective-permute-start(f32[64,256]{1,0:T(8,128)S(1)} %shard_map.142.rest_0_), channel_id=1, source_target_pairs={{0,2},{1,3},{2,0},{3,1},{4,6},{5,7},{6,4},{7,5},{8,10},{9,11},{10,... | collective-permute-start | bytes 196616 | tf_op jit(solution)/shard_map/ppermute | solution.py:276
  26.5 10.9 %collective-permute-start.3 = (f32[256,256]{1,0:T(8,128)}, f32[256,256]{1,0:T(8,128)S(1)}, u32[]{:S(2)}, u32[]{:S(2)}) collective-permute-start(f32[256,256]{1,0:T(8,128)} %get-tuple-element.27), channel_id=1, source_target_pairs={{0,8},{8,0},{16,24},{24,16},{1,9},{9,1},{17,25},{25,17},{2,10},{10... | collective-permute-start | bytes 786440 | tf_op jit(solution)/shard_map/ppermute | solution.py:273
  27.1 12.5 %collective-permute-start.4 = (f32[256,256]{1,0:T(8,128)}, f32[256,256]{1,0:T(8,128)S(1)}, u32[]{:S(2)}, u32[]{:S(2)}) collective-permute-start(f32[256,256]{1,0:T(8,128)} %get-tuple-element.27), channel_id=1, source_target_pairs={{0,16},{8,24},{16,0},{24,8},{1,17},{9,25},{17,1},{25,9},{2,18},{10... | collective-permute-start | bytes 786440 | tf_op jit(solution)/shard_map/ppermute | solution.py:273
  27.6 12.1 %collective-permute-start.5 = (f32[256,256]{1,0:T(8,128)}, f32[256,256]{1,0:T(8,128)S(1)}, u32[]{:S(2)}, u32[]{:S(2)}) collective-permute-start(f32[256,256]{1,0:T(8,128)} %get-tuple-element.27), channel_id=1, source_target_pairs={{0,24},{8,16},{16,8},{24,0},{1,25},{9,17},{17,9},{25,1},{2,26},{10... | collective-permute-start | bytes 786440 | tf_op jit(solution)/shard_map/ppermute | solution.py:273
  36.1 5.4 %collective-permute-start.14 = (f32[64,256]{1,0:T(8,128)S(1)}, f32[64,256]{1,0:T(8,128)S(1)}, u32[]{:S(2)}, u32[]{:S(2)}) collective-permute-start(f32[64,256]{1,0:T(8,128)S(1)} %shard_map.149.rest_0_), channel_id=1, source_target_pairs={{0,8},{8,0},{16,24},{24,16},{1,9},{9,1},{17,25},{25,17},{2,10},{10... | collective-permute-start | bytes 196616 | tf_op jit(solution)/shard_map/ppermute | solution.py:273
  37.4 5.2 %collective-permute-start.16 = (f32[64,256]{1,0:T(8,128)S(1)}, f32[64,256]{1,0:T(8,128)S(1)}, u32[]{:S(2)}, u32[]{:S(2)}) collective-permute-start(f32[64,256]{1,0:T(8,128)S(1)} %shard_map.149.rest_0_), channel_id=1, source_target_pairs={{0,24},{8,16},{16,8},{24,0},{1,25},{9,17},{17,9},{25,1},{2,26},{10... | collective-permute-start | bytes 196616 | tf_op jit(solution)/shard_map/ppermute | solution.py:273
  45.7 5.2 %collective-permute-start.22 = (f32[64,256]{1,0:T(8,128)S(1)}, f32[64,256]{1,0:T(8,128)S(1)}, u32[]{:S(2)}, u32[]{:S(2)}) collective-permute-start(f32[64,256]{1,0:T(8,128)S(1)} %get-tuple-element.37), channel_id=1, source_target_pairs={{0,24},{8,16},{16,8},{24,0},{1,25},{9,17},{17,9},{25,1},{2,26},{10... | collective-permute-start | bytes 196616 | tf_op jit(solution)/shard_map/ppermute | solution.py:273
  50.9 6.1 %collective-permute-start.23 = (f32[64,256]{1,0:T(8,128)S(1)}, f32[64,256]{1,0:T(8,128)S(1)}, u32[]{:S(2)}, u32[]{:S(2)}) collective-permute-start(f32[64,256]{1,0:T(8,128)S(1)} %shard_map.156.rest_0_), channel_id=1, source_target_pairs={{0,2},{1,3},{2,0},{3,1},{4,6},{5,7},{6,4},{7,5},{8,10},{9,11},{10,... | collective-permute-start | bytes 196616 | tf_op jit(solution)/shard_map/ppermute | solution.py:276
  51.0 8.2 %collective-permute-start.24 = (f32[64,256]{1,0:T(8,128)S(1)}, f32[64,256]{1,0:T(8,128)S(1)}, u32[]{:S(2)}, u32[]{:S(2)}) collective-permute-start(f32[64,256]{1,0:T(8,128)S(1)} %shard_map.156.rest_0_), channel_id=1, source_target_pairs={{0,4},{1,5},{2,6},{3,7},{4,0},{5,1},{6,2},{7,3},{8,12},{9,13},{10,... | collective-permute-start | bytes 196616 | tf_op jit(solution)/shard_map/ppermute | solution.py:276
  53.8 6.1 %collective-permute-start.25 = (f32[64,256]{1,0:T(8,128)S(1)}, f32[64,256]{1,0:T(8,128)S(1)}, u32[]{:S(2)}, u32[]{:S(2)}) collective-permute-start(f32[64,256]{1,0:T(8,128)S(1)} %shard_map.156.rest_0_), channel_id=1, source_target_pairs={{0,6},{1,7},{2,4},{3,5},{4,2},{5,3},{6,0},{7,1},{8,14},{9,15},{10,... | collective-permute-start | bytes 196616 | tf_op jit(solution)/shard_map/ppermute | solution.py:276
  55.7 9.5 %collective-permute-start.17 = (f32[256,256]{1,0:T(8,128)S(1)}, f32[256,256]{1,0:T(8,128)S(1)}, u32[]{:S(2)}, u32[]{:S(2)}) collective-permute-start(f32[256,256]{1,0:T(8,128)S(1)} %shard_map.150), channel_id=1, source_target_pairs={{0,8},{8,0},{16,24},{24,16},{1,9},{9,1},{17,25},{25,17},{2,10},{10... | collective-permute-start | bytes 786440 | tf_op jit(solution)/shard_map/ppermute | solution.py:273
  56.3 10.2 %collective-permute-start.18 = (f32[256,256]{1,0:T(8,128)S(1)}, f32[256,256]{1,0:T(8,128)S(1)}, u32[]{:S(2)}, u32[]{:S(2)}) collective-permute-start(f32[256,256]{1,0:T(8,128)S(1)} %shard_map.150), channel_id=1, source_target_pairs={{0,16},{8,24},{16,0},{24,8},{1,17},{9,25},{17,1},{25,9},{2,18},{10... | collective-permute-start | bytes 786440 | tf_op jit(solution)/shard_map/ppermute | solution.py:273
  57.1 9.6 %collective-permute-start.19 = (f32[256,256]{1,0:T(8,128)S(1)}, f32[256,256]{1,0:T(8,128)S(1)}, u32[]{:S(2)}, u32[]{:S(2)}) collective-permute-start(f32[256,256]{1,0:T(8,128)S(1)} %shard_map.150), channel_id=1, source_target_pairs={{0,24},{8,16},{16,8},{24,0},{1,25},{9,17},{17,9},{25,1},{2,26},{10... | collective-permute-start | bytes 786440 | tf_op jit(solution)/shard_map/ppermute | solution.py:273
  63.0 5.1 %collective-permute-start.28 = (f32[64,256]{1,0:T(8,128)S(1)}, f32[64,256]{1,0:T(8,128)S(1)}, u32[]{:S(2)}, u32[]{:S(2)}) collective-permute-start(f32[64,256]{1,0:T(8,128)S(1)} %shard_map.158.rest_0_), channel_id=1, source_target_pairs={{0,8},{8,0},{16,24},{24,16},{1,9},{9,1},{17,25},{25,17},{2,10},{10... | collective-permute-start | bytes 196616 | tf_op jit(solution)/shard_map/ppermute | solution.py:273
  64.0 5.0 %collective-permute-start.29 = (f32[64,256]{1,0:T(8,128)S(1)}, f32[64,256]{1,0:T(8,128)S(1)}, u32[]{:S(2)}, u32[]{:S(2)}) collective-permute-start(f32[64,256]{1,0:T(8,128)S(1)} %shard_map.158.rest_0_), channel_id=1, source_target_pairs={{0,16},{8,24},{16,0},{24,8},{1,17},{9,25},{17,1},{25,9},{2,18},{10... | collective-permute-start | bytes 196616 | tf_op jit(solution)/shard_map/ppermute | solution.py:273
  65.2 5.2 %collective-permute-start.30 = (f32[64,256]{1,0:T(8,128)S(1)}, f32[64,256]{1,0:T(8,128)S(1)}, u32[]{:S(2)}, u32[]{:S(2)}) collective-permute-start(f32[64,256]{1,0:T(8,128)S(1)} %shard_map.158.rest_0_), channel_id=1, source_target_pairs={{0,24},{8,16},{16,8},{24,0},{1,25},{9,17},{17,9},{25,1},{2,26},{10... | collective-permute-start | bytes 196616 | tf_op jit(solution)/shard_map/ppermute | solution.py:273
  (20 other events, 154.8 us)
where the time goes:
time: 71.8 us; the launch traced here: 71.6 us
  starting transfers between devices  38.8 us (54%)
  waiting for transfers between devices  16 us (22%)
  Pallas kernels  14.2 us (20%)
  local copies, waits for them, and re-layouts  1.6 us (2%)
  between operations  0.98 us (1%)
    ppermute x21, starting transfers between devices, sib_from(): return lax.ppermute(value, 'sib', [(i, i ^ o) for i in range(count)])  28.2 us
    pallas_call x20, Pallas kernels, call(): pl.pallas_call(kernel, in_specs=specs, out_specs=tuple((VMEM for _ in out...  14.2 us
    ppermute x21, waiting for transfers between devices, sib_from(): return lax.ppermute(value, 'sib', [(i, i ^ o) for i in range(count)])  11.4 us
    ppermute x10, starting transfers between devices, wide_from(): return lax.ppermute(value, 'wide', [(i, i ^ k) for i in range(wide)])  10.6 us
    ppermute x10, waiting for transfers between devices, wide_from(): return lax.ppermute(value, 'wide', [(i, i ^ k) for i in range(wide)])  4.68 us
    unnamed x26, local copies, waits for them, and re-layouts  1.6 us
  transfers between devices with their start and end apart: 31, of which 13 were waited for; matrix products, arithmetic and copies ran while one was open for 0% of the time, Pallas kernels for 18%

commit v1 on v0

--- a/solution.py
+++ b/solution.py
@@ -15,7 +15,7 @@
 
 
 GRANT = 24 * 1024 * 1024
-LARGE = 61 * 1024 * 1024
+LARGE = 53 * 1024 * 1024
 
 f32 = jnp.float32
 bf16 = jnp.bfloat16
@@ -80,8 +80,8 @@
 
 
 def start_kernel(count, *refs):
-    loads, (xs_ref, ab_ref, *outs) = refs[:4], refs[4 : 6 + count]
-    term, *held, done = refs[6 + count :]
+    loads, (basis_out, trans_out, xs_ref, ab_ref, *outs) = refs[:4], refs[4 : 8 + count]
+    term, *held, done = refs[8 + count :]
     copies = [pltpu.make_async_copy(*ends, done.at[k]) for k, ends in enumerate(zip(loads, held))]
     for copy in copies:
         copy.start()
@@ -95,6 +95,8 @@
     ab_ref[...] = ab
     term[...] = mm(halves(ab), halves(trans_ref[0, 0]))
     send_quarters(term, count, outs)
+    basis_out[...] = basis_ref[...]
+    trans_out[...] = trans_ref[...]
 
 
 def local_kernel(xs_ref, dense_ref, deriv_ref, base_ref):
@@ -122,11 +124,15 @@
         for row in range(0, ref.shape[0], out.shape[0]):
             held[at] = ref[row : row + out.shape[0]]
             at += 1
+    apart = lax.bitwise_xor(partners_ref[...], jnp.full(partners_ref.shape, me, jnp.int32))
+    slots = (apart & 1) * (wide // 2) + (apart >> 1)
     chosen = []
     for k in range(partners_ref.shape[1]):
-        apart = lax.bitwise_xor(partners_ref[0, k], me)
-        slot = lax.rem(apart, 2) * (wide // 2) + lax.div(apart, 2)
-        chosen.append(held[slot])
+        slot = jnp.broadcast_to(slots[:, k : k + 1], out.shape)
+        value = held[0]
+        for j in range(1, wide):
+            value = jnp.where(slot == j, held[j], value)
+        chosen.append(value)
     part = out.shape[0] // 2
     pair = halves(jnp.concatenate(chosen, axis=1))
     depth = pair[0].shape[1]
@@ -150,7 +156,7 @@
     total = None
     extra = None
     for o in range(1, count):
-        parts = [ref[...] for ref in pieces[o - 1]]
+        parts = [ref[:rhs] if len(pieces[o - 1]) > 1 else ref[...] for ref in pieces[o - 1]]
         value = parts[0] if len(parts) == 1 else jnp.concatenate(parts, axis=0)
         slot = lax.rem(peer(o) - me - 1 + count, count)
         pair = halves(value)
@@ -173,12 +179,32 @@
             pick[pl.ds(o * rows + at, chunk)] = jnp.where(wanted == at, 1.0, 0.0).astype(bf16)
 
 
+def pack_body(right_1_ref, right_2_ref, ab_1_ref, ab_2_ref, out_1, out_2, held):
+    rhs = right_1_ref.shape[0]
+    half = rhs // 2
+    rank = out_1.shape[1]
+    for right_ref, ab_ref, out, row in ((right_1_ref, ab_1_ref, out_1, 0), (right_2_ref, ab_2_ref, out_2, half)):
+        out[:rhs] = ab_ref[2 * row : 2 * row + rhs]
+        held[...] = right_ref[row : row + half, 0, :]
+        for k in range(held.shape[1] // rank):
+            out[rhs + k * half : rhs + (k + 1) * half] = held[:, k * rank : (k + 1) * rank]
+
+
 def order_body(pick, *rest):
     pieces, (out, value) = rest[:-2], rest[-2:]
     rhs = out.shape[0]
+    half = rhs // 2
     rows = pieces[0].shape[-1]
-    for o, ref in enumerate(pieces):
+    whole = [ref for ref in pieces if len(ref.shape) == 3]
+    for o, ref in enumerate(whole):
         value[:, o * rows : (o + 1) * rows] = ref[:, 0, :]
+    for j, ref in enumerate(pieces[len(whole) :]):
+        rank = ref.shape[1]
+        for k in range(rows // rank):
+            column = len(whole) * rows + k * rank
+            value[j * half : (j + 1) * half, column : column + rank] = ref[
+                rhs + k * half : rhs + (k + 1) * half
+            ]
     both = one_pass(jnp.concatenate(halves(value[...]), axis=0), pick[...], ((1,), (0,)))
     out[...] = both[:rhs] + both[rhs:]
 
@@ -287,10 +313,10 @@
         return [got[o] for o in range(1, count)]
 
     loaded = (x_start, tangent_start, leaf_basis, transfer)
-    xs, ab, *terms = call(
+    leaf_basis, transfer, xs, ab, *terms = call(
         functools.partial(start_kernel, count),
         loaded,
-        (points, both) + (quarter,) * count,
+        (leaf_basis.shape, transfer.shape, points, both) + (quarter,) * count,
         unit * (2 * depth + 2),
         scratch=[pltpu.VMEM(both, f32)]
         + [pltpu.VMEM(item.shape, f32) for item in loaded]
@@ -298,7 +324,21 @@
         specs=[HBM] * len(loaded),
         grant=LARGE,
     )
-    got_right = [right_side] + siblings([right_side] * count)
+    packed = count == 4
+    if packed:
+        near_right = [sib_from(right_side, o) for o in (1, 2)]
+        near_ab = [sib_from(ab, o) for o in (1, 2)]
+        corners = call(
+            pack_body,
+            near_right + near_ab,
+            ((rhs + rhs * depth // 2, rank),) * 2,
+            unit // count,
+            scratch=(pltpu.VMEM((rhs // 2, leaf), f32),),
+        )
+        corners = [sib_from(corners[0], 2), sib_from(corners[1], 1)]
+        got_right = [right_side] + near_right + corners
+    else:
+        got_right = [right_side] + siblings([right_side] * count)
     lift, again_weight, term_weight = call(
         weights_body,
         (leaf_basis, transfer),
@@ -322,9 +362,10 @@
             away[k] = wide_from(mine, 2 * k)
         away = [away[k] for k in range(1, wide // 2)]
         twin = wide_from(mine, 1)
-        if not last:
-            mine, ab = lax.optimization_barrier((mine, ab))
-        got_ab = siblings([ab] * count)
+        if packed and step == 0:
+            got_ab, sizes = near_ab + corners, [1, 1, 2]
+        else:
+            got_ab, sizes = siblings([ab] * count), [1] * (count - 1)
         (joined,) = call(join_body, away, (((wide // 2 - 1) * 2 * part, rank),), unit // count)
         twins = wide_from(joined, 1)
         (base,) = call(
@@ -339,7 +380,7 @@
                 scratch=(pltpu.VMEM((rhs, count * leaf), f32),),
             )
         (near,) = call(
-            functools.partial(sibling_body, [1] * (count - 1)),
+            functools.partial(sibling_body, sizes),
             [sibling_kernel, sibling_deriv] + got_ab,
             (both,),
             unit * 3 * (count - 1),
@@ -356,7 +397,6 @@
             (quarter,),
             unit * 3 * partners // count,
             scratch=(pltpu.VMEM((wide,) + quarter, f32),),
-            scalars=1,
         )
         got_field = [field] + siblings([field] * count)
         whole = pltpu.VMEM(both, f32)

time: 71.8 us -> 79.9 us (1.11)
  waiting for transfers between devices: 16 us -> 24.1 us
  Pallas kernels: 14.2 us -> 13.4 us
    ppermute x21, waiting for transfers between devices: 11.4 us -> 22.3 us  [sib_from(): return lax.ppermute(value, 'sib', [(i, i ^ o) for i in range(count)])]
    ppermute x10, waiting for transfers between devices: 4.68 us -> 1.8 us  [wide_from(): return lax.ppermute(value, 'wide', [(i, i ^ k) for i in range(wide)])]
    pallas_call x20 -> x21, Pallas kernels: 14.2 us -> 13.4 us  [call(): pl.pallas_call(kernel, in_specs=specs, out_specs=tuple((VMEM for _ in out...]
    unnamed x26 -> x24, local copies, waits for them, and re-layouts: 1.6 us -> 2.05 us
  transfers between devices with their start and end apart: 31 -> 31, of which waited for: 13 -> 14; matrix products, arithmetic and copies ran while one was open for 0% -> 0% of each run, Pallas kernels for 18% -> 11%
where the time goes in v1:
time: 79.9 us; the launch traced here: 79.6 us
  starting transfers between devices  39 us (49%)
  waiting for transfers between devices  24.1 us (30%)
  Pallas kernels  13.4 us (17%)
  local copies, waits for them, and re-layouts  2.05 us (3%)
  between operations  0.99 us (1%)
    ppermute x21, starting transfers between devices, sib_from(): return lax.ppermute(value, 'sib', [(i, i ^ o) for i in range(count)])  28.8 us
    ppermute x21, waiting for transfers between devices, sib_from(): return lax.ppermute(value, 'sib', [(i, i ^ o) for i in range(count)])  22.3 us
    pallas_call x21, Pallas kernels, call(): pl.pallas_call(kernel, in_specs=specs, out_specs=tuple((VMEM for _ in out...  13.4 us
    ppermute x10, starting transfers between devices, wide_from(): return lax.ppermute(value, 'wide', [(i, i ^ k) for i in range(wide)])  10.2 us
    unnamed x24, local copies, waits for them, and re-layouts  2.05 us
    ppermute x10, waiting for transfers between devices, wide_from(): return lax.ppermute(value, 'wide', [(i, i ^ k) for i in range(wide)])  1.8 us
  transfers between devices with their start and end apart: 31, of which 14 were waited for; matrix products, arithmetic and copies ran while one was open for 0% of the time, Pallas kernels for 11%

profile of v1, /device:TPU:0, one launch (start us, length us, event | category | flops | bytes accessed | tf_op | source)
XLA Modules:
  0.0 79.6 jit_solution(6707889958844480379)
XLA Ops:
  0.6 2.8 %shard_map.140 = (f32[1,1,512,256]{3,2,1,0:T(8,128)}, f32[1,1,256,256]{3,2,1,0:T(8,128)S(1)}, f32[256,512]{1,0:T(8,128)}, f32[256,256]{1,0:T(8,128)S(1)}, f32[64...) custom-call(f32[128,1,512]{2,1,0:T(1,128)} %refs_0_.1, ...), custom_call_target="tpu_custom_call" | custom-call | flops 301989888 | bytes 1310720 | tf_op jit(solution)/shard_map/pallas_call | solution.py:58
  3.4 3.0 %collective-permute-start = (f32[256,256]{1,0:T(8,128)S(1)}, f32[256,256]{1,0:T(8,128)S(1)}, u32[]{:S(2)}, u32[]{:S(2)}) collective-permute-start(f32[256,256]{1,0:T(8,128)S(1)} %get-tuple-element.26), channel_id=1, source_target_pairs={{0,8},{8,0},{16,24},{24,16},{1,9},{9,1},{17,25},{25,17},{2,10},{10... | collective-permute-start | bytes 786440 | tf_op jit(solution)/shard_map/ppermute | solution.py:299
  6.5 1.5 %collective-permute-start.1 = (f32[256,256]{1,0:T(8,128)S(1)}, f32[256,256]{1,0:T(8,128)S(1)}, u32[]{:S(2)}, u32[]{:S(2)}) collective-permute-start(f32[256,256]{1,0:T(8,128)S(1)} %get-tuple-element.26), channel_id=1, source_target_pairs={{0,16},{8,24},{16,0},{24,8},{1,17},{9,25},{17,1},{25,9},{2,18},{10... | collective-permute-start | bytes 786440 | tf_op jit(solution)/shard_map/ppermute | solution.py:299
  8.6 1.9 %collective-permute-start.6 = (f32[64,256]{1,0:T(8,128)S(1)}, f32[64,256]{1,0:T(8,128)S(1)}, u32[]{:S(2)}, u32[]{:S(2)}) collective-permute-start(f32[64,256]{1,0:T(8,128)S(1)} %get-tuple-element.32), channel_id=1, source_target_pairs={{0,8},{8,0},{16,24},{24,16},{1,9},{9,1},{17,25},{25,17},{2,10},{10... | collective-permute-start | bytes 196616 | tf_op jit(solution)/shard_map/ppermute | solution.py:299
  10.5 9.3 %collective-permute-done.6.refs_1_ = f32[64,256]{1,0:T(8,128)S(1)} collective-permute-done((f32[64,256]{1,0:T(8,128)S(1)}, f32[64,256]{1,0:T(8,128)S(1)}, u32[]{:S(2)}, u32[]{:S(2)}) %collective-permute-start.6) | collective-permute-done | bytes 65568 | tf_op jit(solution)/shard_map/ppermute | solution.py:299
  19.8 1.8 %collective-permute-start.7 = (f32[64,256]{1,0:T(8,128)S(1)}, f32[64,256]{1,0:T(8,128)S(1)}, u32[]{:S(2)}, u32[]{:S(2)}) collective-permute-start(f32[64,256]{1,0:T(8,128)S(1)} %get-tuple-element.33), channel_id=1, source_target_pairs={{0,16},{8,24},{16,0},{24,8},{1,17},{9,25},{17,1},{25,9},{2,18},{10... | collective-permute-start | bytes 196616 | tf_op jit(solution)/shard_map/ppermute | solution.py:299
  21.6 2.5 %collective-permute-done.7.refs_2_ = f32[64,256]{1,0:T(8,128)S(1)} collective-permute-done((f32[64,256]{1,0:T(8,128)S(1)}, f32[64,256]{1,0:T(8,128)S(1)}, u32[]{:S(2)}, u32[]{:S(2)}) %collective-permute-start.7) | collective-permute-done | bytes 65568 | tf_op jit(solution)/shard_map/ppermute | solution.py:299
  24.1 2.7 %collective-permute-start.8 = (f32[64,256]{1,0:T(8,128)S(1)}, f32[64,256]{1,0:T(8,128)S(1)}, u32[]{:S(2)}, u32[]{:S(2)}) collective-permute-start(f32[64,256]{1,0:T(8,128)S(1)} %get-tuple-element.34), channel_id=1, source_target_pairs={{0,24},{8,16},{16,8},{24,0},{1,25},{9,17},{17,9},{25,1},{2,26},{10... | collective-permute-start | bytes 196616 | tf_op jit(solution)/shard_map/ppermute | solution.py:299
  26.8 2.5 %collective-permute-done.8.refs_3_ = f32[64,256]{1,0:T(8,128)S(1)} collective-permute-done((f32[64,256]{1,0:T(8,128)S(1)}, f32[64,256]{1,0:T(8,128)S(1)}, u32[]{:S(2)}, u32[]{:S(2)}) %collective-permute-start.8) | collective-permute-done | bytes 65568 | tf_op jit(solution)/shard_map/ppermute | solution.py:299
  29.3 2.9 %collective-permute-start.10 = (f32[64,256]{1,0:T(8,128)S(1)}, f32[64,256]{1,0:T(8,128)S(1)}, u32[]{:S(2)}, u32[]{:S(2)}) collective-permute-start(f32[64,256]{1,0:T(8,128)S(1)} %shard_map.148.rest_0_), channel_id=1, source_target_pairs={{0,4},{1,5},{2,6},{3,7},{4,0},{5,1},{6,2},{7,3},{8,12},{9,13},{10,... | collective-permute-start | bytes 196616 | tf_op jit(solution)/shard_map/ppermute | solution.py:302
  32.2 1.3 %collective-permute-start.11 = (f32[64,256]{1,0:T(8,128)S(1)}, f32[64,256]{1,0:T(8,128)S(1)}, u32[]{:S(2)}, u32[]{:S(2)}) collective-permute-start(f32[64,256]{1,0:T(8,128)S(1)} %shard_map.148.rest_0_), channel_id=1, source_target_pairs={{0,6},{1,7},{2,4},{3,5},{4,2},{5,3},{6,0},{7,1},{8,14},{9,15},{10,... | collective-permute-start | bytes 196616 | tf_op jit(solution)/shard_map/ppermute | solution.py:302
  33.9 1.6 %collective-permute-start.4 = (f32[256,256]{1,0:T(8,128)S(1)}, f32[256,256]{1,0:T(8,128)S(1)}, u32[]{:S(2)}, u32[]{:S(2)}) collective-permute-start(f32[256,256]{1,0:T(8,128)S(1)} %get-tuple-element.27), channel_id=1, source_target_pairs={{0,16},{8,24},{16,0},{24,8},{1,17},{9,25},{17,1},{25,9},{2,18},{10... | collective-permute-start | bytes 786440 | tf_op jit(solution)/shard_map/ppermute | solution.py:299
  35.5 1.5 %collective-permute-start.5 = (f32[256,256]{1,0:T(8,128)S(1)}, f32[256,256]{1,0:T(8,128)S(1)}, u32[]{:S(2)}, u32[]{:S(2)}) collective-permute-start(f32[256,256]{1,0:T(8,128)S(1)} %get-tuple-element.28), channel_id=1, source_target_pairs={{0,8},{8,0},{16,24},{24,16},{1,9},{9,1},{17,25},{25,17},{2,10},{10... | collective-permute-start | bytes 786440 | tf_op jit(solution)/shard_map/ppermute | solution.py:299
  37.0 1.3 %collective-permute-done.11.refs_2_ = f32[64,256]{1,0:T(8,128)S(1)} collective-permute-done((f32[64,256]{1,0:T(8,128)S(1)}, f32[64,256]{1,0:T(8,128)S(1)}, u32[]{:S(2)}, u32[]{:S(2)}) %collective-permute-start.11) | collective-permute-done | bytes 65568 | tf_op jit(solution)/shard_map/ppermute | solution.py:302
  44.1 1.6 %collective-permute-start.14 = (f32[64,256]{1,0:T(8,128)S(1)}, f32[64,256]{1,0:T(8,128)S(1)}, u32[]{:S(2)}, u32[]{:S(2)}) collective-permute-start(f32[64,256]{1,0:T(8,128)S(1)} %shard_map.150.rest_0_), channel_id=1, source_target_pairs={{0,8},{8,0},{16,24},{24,16},{1,9},{9,1},{17,25},{25,17},{2,10},{10... | collective-permute-start | bytes 196616 | tf_op jit(solution)/shard_map/ppermute | solution.py:299
  45.7 1.5 %collective-permute-start.15 = (f32[64,256]{1,0:T(8,128)S(1)}, f32[64,256]{1,0:T(8,128)S(1)}, u32[]{:S(2)}, u32[]{:S(2)}) collective-permute-start(f32[64,256]{1,0:T(8,128)S(1)} %shard_map.150.rest_0_), channel_id=1, source_target_pairs={{0,16},{8,24},{16,0},{24,8},{1,17},{9,25},{17,1},{25,9},{2,18},{10... | collective-permute-start | bytes 196616 | tf_op jit(solution)/shard_map/ppermute | solution.py:299
  50.6 1.7 %collective-permute-done.16.rest_3_ = f32[64,256]{1,0:T(8,128)S(1)} collective-permute-done((f32[64,256]{1,0:T(8,128)S(1)}, f32[64,256]{1,0:T(8,128)S(1)}, u32[]{:S(2)}, u32[]{:S(2)}) %collective-permute-start.16) | collective-permute-done | bytes 65568 | tf_op jit(solution)/shard_map/ppermute | solution.py:299
  54.0 2.2 %collective-permute-start.22 = (f32[64,256]{1,0:T(8,128)S(1)}, f32[64,256]{1,0:T(8,128)S(1)}, u32[]{:S(2)}, u32[]{:S(2)}) collective-permute-start(f32[64,256]{1,0:T(8,128)S(1)} %get-tuple-element.41), channel_id=1, source_target_pairs={{0,24},{8,16},{16,8},{24,0},{1,25},{9,17},{17,9},{25,1},{2,26},{10... | collective-permute-start | bytes 196616 | tf_op jit(solution)/shard_map/ppermute | solution.py:299
  57.8 1.3 %collective-permute-done.22.refs_3_ = f32[64,256]{1,0:T(8,128)S(1)} collective-permute-done((f32[64,256]{1,0:T(8,128)S(1)}, f32[64,256]{1,0:T(8,128)S(1)}, u32[]{:S(2)}, u32[]{:S(2)}) %collective-permute-start.22) | collective-permute-done | bytes 65568 | tf_op jit(solution)/shard_map/ppermute | solution.py:299
  59.3 2.4 %collective-permute-start.24 = (f32[64,256]{1,0:T(8,128)S(1)}, f32[64,256]{1,0:T(8,128)S(1)}, u32[]{:S(2)}, u32[]{:S(2)}) collective-permute-start(f32[64,256]{1,0:T(8,128)S(1)} %shard_map.157.rest_0_), channel_id=1, source_target_pairs={{0,4},{1,5},{2,6},{3,7},{4,0},{5,1},{6,2},{7,3},{8,12},{9,13},{10,... | collective-permute-start | bytes 196616 | tf_op jit(solution)/shard_map/ppermute | solution.py:302
  61.7 1.9 %collective-permute-start.25 = (f32[64,256]{1,0:T(8,128)S(1)}, f32[64,256]{1,0:T(8,128)S(1)}, u32[]{:S(2)}, u32[]{:S(2)}) collective-permute-start(f32[64,256]{1,0:T(8,128)S(1)} %shard_map.157.rest_0_), channel_id=1, source_target_pairs={{0,6},{1,7},{2,4},{3,5},{4,2},{5,3},{6,0},{7,1},{8,14},{9,15},{10,... | collective-permute-start | bytes 196616 | tf_op jit(solution)/shard_map/ppermute | solution.py:302
  65.2 1.5 %collective-permute-start.18 = (f32[256,256]{1,0:T(8,128)S(1)}, f32[256,256]{1,0:T(8,128)S(1)}, u32[]{:S(2)}, u32[]{:S(2)}) collective-permute-start(f32[256,256]{1,0:T(8,128)S(1)} %shard_map.151), channel_id=1, source_target_pairs={{0,16},{8,24},{16,0},{24,8},{1,17},{9,25},{17,1},{25,9},{2,18},{10... | collective-permute-start | bytes 786440 | tf_op jit(solution)/shard_map/ppermute | solution.py:299
  71.7 1.5 %collective-permute-start.29 = (f32[64,256]{1,0:T(8,128)S(1)}, f32[64,256]{1,0:T(8,128)S(1)}, u32[]{:S(2)}, u32[]{:S(2)}) collective-permute-start(f32[64,256]{1,0:T(8,128)S(1)} %shard_map.159.rest_0_), channel_id=1, source_target_pairs={{0,16},{8,24},{16,0},{24,8},{1,17},{9,25},{17,1},{25,9},{2,18},{10... | collective-permute-start | bytes 196616 | tf_op jit(solution)/shard_map/ppermute | solution.py:299
  74.0 1.6 %collective-permute-done.18.rest_1_ = f32[256,256]{1,0:T(8,128)S(1)} collective-permute-done((f32[256,256]{1,0:T(8,128)S(1)}, f32[256,256]{1,0:T(8,128)S(1)}, u32[]{:S(2)}, u32[]{:S(2)}) %collective-permute-start.18) | collective-permute-done | bytes 262176 | tf_op jit(solution)/shard_map/ppermute | solution.py:299
  (83 shorter events, 24.5 us)
Async XLA Ops:
  3.4 28.7 %collective-permute-start = (f32[256,256]{1,0:T(8,128)S(1)}, f32[256,256]{1,0:T(8,128)S(1)}, u32[]{:S(2)}, u32[]{:S(2)}) collective-permute-start(f32[256,256]{1,0:T(8,128)S(1)} %get-tuple-element.26), channel_id=1, source_target_pairs={{0,8},{8,0},{16,24},{24,16},{1,9},{9,1},{17,25},{25,17},{2,10},{10... | collective-permute-start | bytes 786440 | tf_op jit(solution)/shard_map/ppermute | solution.py:299
  6.5 27.0 %collective-permute-start.1 = (f32[256,256]{1,0:T(8,128)S(1)}, f32[256,256]{1,0:T(8,128)S(1)}, u32[]{:S(2)}, u32[]{:S(2)}) collective-permute-start(f32[256,256]{1,0:T(8,128)S(1)} %get-tuple-element.26), channel_id=1, source_target_pairs={{0,16},{8,24},{16,0},{24,8},{1,17},{9,25},{17,1},{25,9},{2,18},{10... | collective-permute-start | bytes 786440 | tf_op jit(solution)/shard_map/ppermute | solution.py:299
  8.0 25.8 %collective-permute-start.2 = (f32[128,1,512]{2,1,0:T(1,128)}, f32[128,1,512]{2,1,0:T(1,128)S(1)}, u32[]{:S(2)}, u32[]{:S(2)}) collective-permute-start(f32[128,1,512]{2,1,0:T(1,128)} %rest_0_.1), channel_id=1, source_target_pairs={{0,8},{8,0},{16,24},{24,16},{1,9},{9,1},{17,25},{25,17},{2,10},{10... | collective-permute-start | bytes 786440 | tf_op jit(solution)/shard_map/ppermute | solution.py:299
  8.5 25.3 %collective-permute-start.3 = (f32[128,1,512]{2,1,0:T(1,128)}, f32[128,1,512]{2,1,0:T(1,128)S(1)}, u32[]{:S(2)}, u32[]{:S(2)}) collective-permute-start(f32[128,1,512]{2,1,0:T(1,128)} %rest_0_.1), channel_id=1, source_target_pairs={{0,16},{8,24},{16,0},{24,8},{1,17},{9,25},{17,1},{25,9},{2,18},{10... | collective-permute-start | bytes 786440 | tf_op jit(solution)/shard_map/ppermute | solution.py:299
  8.6 11.2 %collective-permute-start.6 = (f32[64,256]{1,0:T(8,128)S(1)}, f32[64,256]{1,0:T(8,128)S(1)}, u32[]{:S(2)}, u32[]{:S(2)}) collective-permute-start(f32[64,256]{1,0:T(8,128)S(1)} %get-tuple-element.32), channel_id=1, source_target_pairs={{0,8},{8,0},{16,24},{24,16},{1,9},{9,1},{17,25},{25,17},{2,10},{10... | collective-permute-start | bytes 196616 | tf_op jit(solution)/shard_map/ppermute | solution.py:299
  24.1 5.2 %collective-permute-start.8 = (f32[64,256]{1,0:T(8,128)S(1)}, f32[64,256]{1,0:T(8,128)S(1)}, u32[]{:S(2)}, u32[]{:S(2)}) collective-permute-start(f32[64,256]{1,0:T(8,128)S(1)} %get-tuple-element.34), channel_id=1, source_target_pairs={{0,24},{8,16},{16,8},{24,0},{1,25},{9,17},{17,9},{25,1},{2,26},{10... | collective-permute-start | bytes 196616 | tf_op jit(solution)/shard_map/ppermute | solution.py:299
  29.3 7.7 %collective-permute-start.10 = (f32[64,256]{1,0:T(8,128)S(1)}, f32[64,256]{1,0:T(8,128)S(1)}, u32[]{:S(2)}, u32[]{:S(2)}) collective-permute-start(f32[64,256]{1,0:T(8,128)S(1)} %shard_map.148.rest_0_), channel_id=1, source_target_pairs={{0,4},{1,5},{2,6},{3,7},{4,0},{5,1},{6,2},{7,3},{8,12},{9,13},{10,... | collective-permute-start | bytes 196616 | tf_op jit(solution)/shard_map/ppermute | solution.py:302
  32.2 6.2 %collective-permute-start.11 = (f32[64,256]{1,0:T(8,128)S(1)}, f32[64,256]{1,0:T(8,128)S(1)}, u32[]{:S(2)}, u32[]{:S(2)}) collective-permute-start(f32[64,256]{1,0:T(8,128)S(1)} %shard_map.148.rest_0_), channel_id=1, source_target_pairs={{0,6},{1,7},{2,4},{3,5},{4,2},{5,3},{6,0},{7,1},{8,14},{9,15},{10,... | collective-permute-start | bytes 196616 | tf_op jit(solution)/shard_map/ppermute | solution.py:302
  33.5 5.0 %collective-permute-start.9 = (f32[64,256]{1,0:T(8,128)S(1)}, f32[64,256]{1,0:T(8,128)S(1)}, u32[]{:S(2)}, u32[]{:S(2)}) collective-permute-start(f32[64,256]{1,0:T(8,128)S(1)} %shard_map.148.rest_0_), channel_id=1, source_target_pairs={{0,2},{1,3},{2,0},{3,1},{4,6},{5,7},{6,4},{7,5},{8,10},{9,11},{10,... | collective-permute-start | bytes 196616 | tf_op jit(solution)/shard_map/ppermute | solution.py:302
  33.9 13.8 %collective-permute-start.4 = (f32[256,256]{1,0:T(8,128)S(1)}, f32[256,256]{1,0:T(8,128)S(1)}, u32[]{:S(2)}, u32[]{:S(2)}) collective-permute-start(f32[256,256]{1,0:T(8,128)S(1)} %get-tuple-element.27), channel_id=1, source_target_pairs={{0,16},{8,24},{16,0},{24,8},{1,17},{9,25},{17,1},{25,9},{2,18},{10... | collective-permute-start | bytes 786440 | tf_op jit(solution)/shard_map/ppermute | solution.py:299
  35.5 12.2 %collective-permute-start.5 = (f32[256,256]{1,0:T(8,128)S(1)}, f32[256,256]{1,0:T(8,128)S(1)}, u32[]{:S(2)}, u32[]{:S(2)}) collective-permute-start(f32[256,256]{1,0:T(8,128)S(1)} %get-tuple-element.28), channel_id=1, source_target_pairs={{0,8},{8,0},{16,24},{24,16},{1,9},{9,1},{17,25},{25,17},{2,10},{10... | collective-permute-start | bytes 786440 | tf_op jit(solution)/shard_map/ppermute | solution.py:299
  44.1 6.5 %collective-permute-start.14 = (f32[64,256]{1,0:T(8,128)S(1)}, f32[64,256]{1,0:T(8,128)S(1)}, u32[]{:S(2)}, u32[]{:S(2)}) collective-permute-start(f32[64,256]{1,0:T(8,128)S(1)} %shard_map.150.rest_0_), channel_id=1, source_target_pairs={{0,8},{8,0},{16,24},{24,16},{1,9},{9,1},{17,25},{25,17},{2,10},{10... | collective-permute-start | bytes 196616 | tf_op jit(solution)/shard_map/ppermute | solution.py:299
  45.7 4.9 %collective-permute-start.15 = (f32[64,256]{1,0:T(8,128)S(1)}, f32[64,256]{1,0:T(8,128)S(1)}, u32[]{:S(2)}, u32[]{:S(2)}) collective-permute-start(f32[64,256]{1,0:T(8,128)S(1)} %shard_map.150.rest_0_), channel_id=1, source_target_pairs={{0,16},{8,24},{16,0},{24,8},{1,17},{9,25},{17,1},{25,9},{2,18},{10... | collective-permute-start | bytes 196616 | tf_op jit(solution)/shard_map/ppermute | solution.py:299
  47.2 5.2 %collective-permute-start.16 = (f32[64,256]{1,0:T(8,128)S(1)}, f32[64,256]{1,0:T(8,128)S(1)}, u32[]{:S(2)}, u32[]{:S(2)}) collective-permute-start(f32[64,256]{1,0:T(8,128)S(1)} %shard_map.150.rest_0_), channel_id=1, source_target_pairs={{0,24},{8,16},{16,8},{24,0},{1,25},{9,17},{17,9},{25,1},{2,26},{10... | collective-permute-start | bytes 196616 | tf_op jit(solution)/shard_map/ppermute | solution.py:299
  54.0 5.2 %collective-permute-start.22 = (f32[64,256]{1,0:T(8,128)S(1)}, f32[64,256]{1,0:T(8,128)S(1)}, u32[]{:S(2)}, u32[]{:S(2)}) collective-permute-start(f32[64,256]{1,0:T(8,128)S(1)} %get-tuple-element.41), channel_id=1, source_target_pairs={{0,24},{8,16},{16,8},{24,0},{1,25},{9,17},{17,9},{25,1},{2,26},{10... | collective-permute-start | bytes 196616 | tf_op jit(solution)/shard_map/ppermute | solution.py:299
  59.2 7.6 %collective-permute-start.23 = (f32[64,256]{1,0:T(8,128)S(1)}, f32[64,256]{1,0:T(8,128)S(1)}, u32[]{:S(2)}, u32[]{:S(2)}) collective-permute-start(f32[64,256]{1,0:T(8,128)S(1)} %shard_map.157.rest_0_), channel_id=1, source_target_pairs={{0,2},{1,3},{2,0},{3,1},{4,6},{5,7},{6,4},{7,5},{8,10},{9,11},{10,... | collective-permute-start | bytes 196616 | tf_op jit(solution)/shard_map/ppermute | solution.py:302
  59.3 8.2 %collective-permute-start.24 = (f32[64,256]{1,0:T(8,128)S(1)}, f32[64,256]{1,0:T(8,128)S(1)}, u32[]{:S(2)}, u32[]{:S(2)}) collective-permute-start(f32[64,256]{1,0:T(8,128)S(1)} %shard_map.157.rest_0_), channel_id=1, source_target_pairs={{0,4},{1,5},{2,6},{3,7},{4,0},{5,1},{6,2},{7,3},{8,12},{9,13},{10,... | collective-permute-start | bytes 196616 | tf_op jit(solution)/shard_map/ppermute | solution.py:302
  61.7 6.1 %collective-permute-start.25 = (f32[64,256]{1,0:T(8,128)S(1)}, f32[64,256]{1,0:T(8,128)S(1)}, u32[]{:S(2)}, u32[]{:S(2)}) collective-permute-start(f32[64,256]{1,0:T(8,128)S(1)} %shard_map.157.rest_0_), channel_id=1, source_target_pairs={{0,6},{1,7},{2,4},{3,5},{4,2},{5,3},{6,0},{7,1},{8,14},{9,15},{10,... | collective-permute-start | bytes 196616 | tf_op jit(solution)/shard_map/ppermute | solution.py:302
  63.9 9.3 %collective-permute-start.17 = (f32[256,256]{1,0:T(8,128)S(1)}, f32[256,256]{1,0:T(8,128)S(1)}, u32[]{:S(2)}, u32[]{:S(2)}) collective-permute-start(f32[256,256]{1,0:T(8,128)S(1)} %shard_map.151), channel_id=1, source_target_pairs={{0,8},{8,0},{16,24},{24,16},{1,9},{9,1},{17,25},{25,17},{2,10},{10... | collective-permute-start | bytes 786440 | tf_op jit(solution)/shard_map/ppermute | solution.py:299
  65.2 10.4 %collective-permute-start.18 = (f32[256,256]{1,0:T(8,128)S(1)}, f32[256,256]{1,0:T(8,128)S(1)}, u32[]{:S(2)}, u32[]{:S(2)}) collective-permute-start(f32[256,256]{1,0:T(8,128)S(1)} %shard_map.151), channel_id=1, source_target_pairs={{0,16},{8,24},{16,0},{24,8},{1,17},{9,25},{17,1},{25,9},{2,18},{10... | collective-permute-start | bytes 786440 | tf_op jit(solution)/shard_map/ppermute | solution.py:299
  66.8 8.8 %collective-permute-start.19 = (f32[256,256]{1,0:T(8,128)S(1)}, f32[256,256]{1,0:T(8,128)S(1)}, u32[]{:S(2)}, u32[]{:S(2)}) collective-permute-start(f32[256,256]{1,0:T(8,128)S(1)} %shard_map.151), channel_id=1, source_target_pairs={{0,24},{8,16},{16,8},{24,0},{1,25},{9,17},{17,9},{25,1},{2,26},{10... | collective-permute-start | bytes 786440 | tf_op jit(solution)/shard_map/ppermute | solution.py:299
  70.4 6.8 %collective-permute-start.28 = (f32[64,256]{1,0:T(8,128)S(1)}, f32[64,256]{1,0:T(8,128)S(1)}, u32[]{:S(2)}, u32[]{:S(2)}) collective-permute-start(f32[64,256]{1,0:T(8,128)S(1)} %shard_map.159.rest_0_), channel_id=1, source_target_pairs={{0,8},{8,0},{16,24},{24,16},{1,9},{9,1},{17,25},{25,17},{2,10},{10... | collective-permute-start | bytes 196616 | tf_op jit(solution)/shard_map/ppermute | solution.py:299
  71.7 5.9 %collective-permute-start.29 = (f32[64,256]{1,0:T(8,128)S(1)}, f32[64,256]{1,0:T(8,128)S(1)}, u32[]{:S(2)}, u32[]{:S(2)}) collective-permute-start(f32[64,256]{1,0:T(8,128)S(1)} %shard_map.159.rest_0_), channel_id=1, source_target_pairs={{0,16},{8,24},{16,0},{24,8},{1,17},{9,25},{17,1},{25,9},{2,18},{10... | collective-permute-start | bytes 196616 | tf_op jit(solution)/shard_map/ppermute | solution.py:299
  73.2 5.2 %collective-permute-start.30 = (f32[64,256]{1,0:T(8,128)S(1)}, f32[64,256]{1,0:T(8,128)S(1)}, u32[]{:S(2)}, u32[]{:S(2)}) collective-permute-start(f32[64,256]{1,0:T(8,128)S(1)} %shard_map.159.rest_0_), channel_id=1, source_target_pairs={{0,24},{8,16},{16,8},{24,0},{1,25},{9,17},{17,9},{25,1},{2,26},{10... | collective-permute-start | bytes 196616 | tf_op jit(solution)/shard_map/ppermute | solution.py:299
  (19 other events, 107.5 us)
